TPU v7x, 32 devices: a whole 2x2x4 slice. The times are simulated.
32 devices in a mesh: section: 2 (over core), seq: 4 (over y, x), head: 4 (over z).
Axes of the slice: x: 2, y: 2, z: 4, core: 2. Of those that a mesh axis runs over, the one named last changes fastest.
Arguments:
- x_in: bfloat16 [2, 1024, 8192], P('section', 'seq', 'head'), may hold values from -6 to 6
- b_in: bfloat16 [2, 1024, 2048], P('section', 'seq', 'head'), may hold values from -6 to 6
- c_in: bfloat16 [2, 1024, 2048], P('section', 'seq', 'head'), may hold values from -6 to 6
- z_in: bfloat16 [2, 1024, 8192], P('section', 'seq', 'head'), may hold values from -6 to 6
- dt_raw: float32 [2, 128, 1024], P('section', 'head', 'seq'), may hold values from -5 to 5
- conv_x: float32 [2, 4, 8192], P('section', None, 'head'), may hold values from -3 to 3
- conv_b: float32 [2, 4, 2048], P('section', None, 'head'), may hold values from -3 to 3
- conv_c: float32 [2, 4, 2048], P('section', None, 'head'), may hold values from -3 to 3
- a_rate: float32 [2, 128], P('section', 'head'), may hold values from 0.0001 to 1
- dt_bias: float32 [2, 128], P('section', 'head'), may hold values from -3 to -0.5
- skip_d: float32 [2, 128], P('section', 'head'), may hold values from 0.5 to 2
- norm_gain: float32 [2, 8192], P('section', 'head'), may hold values from 0.25 to 1.75
- out_weight: bfloat16 [2, 8192, 8192], P('section', 'head', 'seq'), may hold values from -0.0625 to 0.0625
Outputs:
- mixed: bfloat16 [2, 1024, 8192], P('section', ('seq', 'head'))
All inputs are finite; a program needn't handle non-finite values.
Results may differ from a plain program's by a relative error of at most 0.007.
Values may be sent and summed in bfloat16 or wider, within the bound.
A program may use at most 128 MiB of HBM per device.

v0:
```python
import jax
import jax.numpy as jnp
from jax import lax
from jax.sharding import PartitionSpec as P

N = 256
epsilon = 1e-05


def passed_along(block, axis, distance):
    devices = range(lax.axis_size(axis))
    route = [(i - distance, i) for i in devices if i - distance in devices]
    return lax.ppermute(block, axis, route)


def entering(decay, block, axis):
    size, place = (lax.axis_size(axis), lax.axis_index(axis))
    decays = lax.all_gather(decay, axis)
    blocks = lax.all_gather(block.astype(jnp.bfloat16), axis)
    carried = jnp.zeros_like(block)
    for k in range(size - 1):
        after = decays[k][:, :, None, None] * carried + blocks[k].astype(jnp.float32)
        carried = jnp.where(k < place, after, carried)
    return carried


def passed_along_2(block, axis, distance):
    devices = range(lax.axis_size(axis))
    route = [((i - distance) % len(devices), i) for i in devices]
    return lax.ppermute(block, axis, route)


def conv_silu(padded, kernel, length):
    kernel_taps = kernel.shape[0]
    summed = jnp.zeros((length, padded.shape[1]), jnp.float32)
    for offset in range(kernel_taps):
        summed = summed + kernel[offset] * padded[offset : offset + length].astype(jnp.float32)
    return jax.nn.silu(summed).astype(jnp.bfloat16)


def per_device(
    x_in,
    b_in,
    c_in,
    z_in,
    dt_raw,
    conv_x,
    conv_b,
    conv_c,
    a_rate,
    dt_bias,
    skip_d,
    norm_gain,
    out_weight,
):
    x_local = x_in[0]
    b_local = b_in[0]
    c_local = c_in[0]
    length = x_local.shape[0]
    kernel_taps = conv_x.shape[1]
    x_cols = x_local.shape[1]
    b_cols = b_local.shape[1]
    edge_rows = jnp.concatenate(
        [
            x_local[length - kernel_taps + 1 :],
            b_local[length - kernel_taps + 1 :],
            c_local[length - kernel_taps + 1 :],
        ],
        axis=1,
    )
    before = passed_along(edge_rows, "seq", 1)
    x_conv = conv_silu(jnp.concatenate([before[:, :x_cols], x_local], axis=0), conv_x[0], length)
    b_conv = conv_silu(
        jnp.concatenate([before[:, x_cols : x_cols + b_cols], b_local], axis=0), conv_b[0], length
    )
    c_conv = conv_silu(
        jnp.concatenate([before[:, x_cols + b_cols :], c_local], axis=0), conv_c[0], length
    )
    head_count = dt_raw.shape[1]
    group_count = b_cols // N
    per_group = head_count // group_count
    head_dim = x_cols // head_count
    step_size = jax.nn.softplus(dt_raw[0] + dt_bias[0][:, None])
    log_decay = jnp.cumsum(-a_rate[0][:, None] * step_size, axis=1)
    x_groups = x_conv.reshape(length, group_count, per_group, head_dim)
    b_groups = b_conv.reshape(length, group_count, N)
    c_groups = c_conv.reshape(length, group_count, N)
    log_groups = log_decay.reshape(group_count, per_group, length)
    step_groups = step_size.reshape(group_count, per_group, length)
    scores = jnp.einsum("tgn,ugn->gtu", c_groups, b_groups, preferred_element_type=jnp.float32)
    causal = jnp.arange(length)[:, None] >= jnp.arange(length)[None, :]
    spread_log = log_groups[:, :, :, None] - log_groups[:, :, None, :]
    damping = jnp.where(causal, jnp.exp(jnp.minimum(spread_log, 0.0)), 0.0)
    weights = (damping * step_groups[:, :, None, :] * scores[:, None]).astype(jnp.bfloat16)
    inside = jnp.einsum("gjtu,ugjp->tgjp", weights, x_groups, preferred_element_type=jnp.float32)
    to_end = jnp.exp(log_groups[:, :, -1:] - log_groups) * step_groups
    x_weighted = (
        x_groups.astype(jnp.float32) * jnp.transpose(to_end, (2, 0, 1))[..., None]
    ).astype(jnp.bfloat16)
    block_sum = jnp.einsum(
        "ugjp,ugn->gjpn", x_weighted, b_groups, preferred_element_type=jnp.float32
    )
    block_decay = jnp.exp(log_groups[:, :, -1])
    carried = entering(block_decay, block_sum, "seq")
    carried_b = carried.astype(jnp.bfloat16)
    outside = jnp.einsum("tgn,gjpn->tgjp", c_groups, carried_b, preferred_element_type=jnp.float32)
    outside = outside * jnp.transpose(jnp.exp(log_groups), (2, 0, 1))[..., None]
    skip_term = skip_d[0].reshape(group_count, per_group)
    out_ssm = inside + outside + skip_term[None, :, :, None] * x_groups.astype(jnp.float32)
    gate_act = jax.nn.silu(z_in[0].astype(jnp.float32)).reshape(
        length, group_count, per_group * head_dim
    )
    gated = out_ssm.reshape(length, group_count, per_group * head_dim) * gate_act
    inverse_rms = lax.rsqrt(jnp.mean(gated * gated, axis=2, keepdims=True) + epsilon)
    hidden = ((gated * inverse_rms).reshape(length, x_cols) * norm_gain[0]).astype(jnp.bfloat16)
    local_weight = out_weight[0]
    terms = jnp.dot(
        lax.all_gather(hidden, "seq", axis=0, tiled=True),
        local_weight,
        preferred_element_type=jnp.float32,
    )
    shards = lax.axis_size("seq")
    terms = terms.astype(jnp.bfloat16).reshape(shards, length, local_weight.shape[1])
    summed = lax.psum_scatter(terms, "head", scatter_dimension=1, tiled=True)
    spread = lax.all_to_all(summed, "seq", split_axis=0, concat_axis=2, tiled=True)
    mixed = spread.reshape(spread.shape[1], spread.shape[2])
    passed = passed_along_2(mixed, "section", 1)
    return passed[None]


def solution(mesh):
    return jax.shard_map(
        per_device,
        mesh=mesh,
        in_specs=(
            P("section", "seq", "head"),
            P("section", "seq", "head"),
            P("section", "seq", "head"),
            P("section", "seq", "head"),
            P("section", "head", "seq"),
            P("section", None, "head"),
            P("section", None, "head"),
            P("section", None, "head"),
            P("section", "head"),
            P("section", "head"),
            P("section", "head"),
            P("section", "head"),
            P("section", "head", "seq"),
        ),
        out_specs=P("section", ("seq", "head"), None),
        check_vma=False,
    )
```

profile of v0, /device:TPU:0, one launch (start us, length us, event | category | flops | bytes accessed | tf_op | source)
XLA Modules:
  0.0 265.6 jit_solution(9218574246040160207)
XLA Ops:
  6.5 0.9 slice_bitcast_fusion
  7.4 0.7 slice_bitcast_fusion.1
  8.1 4.9 %collective-permute-start = (bf16[3,3072]{1,0:T(4,128)(2,1)S(1)}, bf16[3,3072]{1,0:T(4,128)(2,1)S(1)}, u32[]{:S(2)}, u32[]{:S(2)}) collective-permute-start(bf16[3,3072]{1,0:T(4,128)(2,1)S(1)} %pad_maximum_fusion.3), channel_id=1, source_target_pairs={{0,4},{4,8},{8,12},{1,5},{5,9},{9,13},{2,6},{6,10},{10,14},{3,7},{... | collective-permute-start | bytes 55304 | tf_op jit(solution)/shard_map/ppermute | solution.py:13
  13.0 0.7 negate_bitcast_fusion
  14.2 1.3 reduce.9
  15.6 0.8 squeeze.26
  16.3 0.7 fusion.47
  17.1 0.6 reduce-window.6
  18.2 0.9 fusion.50
  19.2 1.4 multiply_bitcast_fusion
  20.6 0.9 fusion.53
  21.4 1.9 multiply_convert_fusion.5
  23.5 1.5 multiply_convert_fusion.2
  25.5 1.4 convolution_convert_fusion
  27.1 0.6 reduce.10
  27.8 1.6 copy.67
  29.4 8.1 %all-gather = f32[8,16,1]{1,2,0:T(1,128)S(1)} all-gather(f32[2,16,1]{1,2,0:T(1,128)S(1)} %bitcast.125), channel_id=2, replica_groups=mesh['section'=2,'seq'=4,'head'=4] {'seq'}, dimensions={0}, use_global_device_ids=true | all-gather | bytes 640 | tf_op jit(solution)/shard_map/all_gather | solution.py:18
  38.2 41.8 %all-gather.7.cloned.1.call-done = bf16[8,16,64,256]{3,2,1,0:T(8,128)(2,1)} async-done(((bf16[2,16,64,256]{3,2,1,0:T(8,128)(2,1)}), bf16[8,16,64,256]{3,2,1,0:T(8,128)(2,1)}) %all-gather.7.cloned.1.call-update) | async-done | bytes 4194320 | tf_op jit(solution)/shard_map/all_gather | solution.py:19
  80.0 3.0 %fusion.31 = f32[2,16,64,256]{3,2,1,0:T(8,128)S(1)} fusion(bf16[8,16,64,256]{3,2,1,0:T(8,128)(2,1)} %all-gather.7.cloned.1.call-done, f32[2,16]{1,0:T(2,128)S(1)} %bitcast.128, f32[2,16]{1,0:T(2,128)S(1)} %bitcast.127, f32[2,16]{1,0:T(2,128)S(1)} %bitcast.126, pred[]{:T(512)S(6)} %gt.11, pred[]{:T(512)S(6)} %gt.10, pred[]{:T(512)S(6)} %gt.9, ...), kind=kOutput, calls=%fused_computation.43 | convolution fusion | flops 274726912 | bytes 5505411 | tf_op jit(solution)/shard_map/tgn,gjpn->tgjp/dot_general | solution.py:106
  83.0 4.5 %multiply_reduce_fusion = (f32[256,2]{0,1:T(2,128)S(1)}, f32[256,2,16,64]{0,3,2,1:T(8,128)}) fusion(f32[256,2,16,64]{0,3,2,1:T(8,128)S(1)} %bitcast.99, bf16[256,2,16,64]{0,3,2,1:T(8,128)(2,1)S(1)} %bitcast.103, f32[2,16]{1,0:T(2,128)S(1)} %mul.316, f32[256,2,16]{0,2,1:T(8,128)S(1)} %copy-done.4, f32[2,16,64,256]{3,2,1,0:T(8,128)S(1)} %fusion.31, ...), kind=kOutput, calls=%fused_computation.33 | convolution fusion | flops 287309312 | bytes 8030336 | tf_op jit(solution)/shard_map/gjtu,ugjp->tgjp/dot_general | solution.py:95
  87.5 1.9 copy.66
  89.6 0.6 mul.324
  90.2 0.9 copy.79
  91.1 1.8 fusion.26
  92.9 52.7 %all-gather.5.cloned.1.call-done = bf16[1024,2048]{1,0:T(8,128)(2,1)} async-done(((bf16[256,2048]{1,0:T(8,128)(2,1)}), bf16[1024,2048]{1,0:T(8,128)(2,1)}) %all-gather.5.cloned.1.call-update) | async-done | bytes 4194320 | tf_op jit(solution)/shard_map/all_gather | solution.py:118
  145.6 13.8 %fusion.9 = bf16[1024,2048]{1,0:T(8,128)(2,1)} fusion(bf16[1024,2048]{1,0:T(8,128)(2,1)} %all-gather.5.cloned.1.call-done, bf16[1,2048,2048]{2,1,0:T(8,128)(2,1)} %param.25), kind=kOutput, calls=%fused_computation.10 | convolution fusion | flops 8592031744 | bytes 16777216 | tf_op jit(solution)/shard_map/dot_general | solution.py:117
  159.4 77.0 %reduce-scatter.2.cloned.1.call-done = bf16[4,64,2048]{2,1,0:T(8,128)(2,1)} async-done(((bf16[4,256,2048]{2,1,0:T(8,128)(2,1)}), bf16[4,64,2048]{2,1,0:T(8,128)(2,1)}) %reduce-scatter.2.cloned.1.call-update) | async-done | bytes 1048592 | tf_op jit(solution)/shard_map/reduce_scatter | solution.py:124
  236.4 17.6 %all_to_all.15 = bf16[4,64,2048]{2,1,0:T(8,128)(2,1)S(1)} all-to-all(bf16[4,64,2048]{2,1,0:T(8,128)(2,1)} %reduce-scatter.2.cloned.1.call-done), channel_id=1, replica_groups=mesh['section'=2,'seq'=4,'head'=4] {'seq'}, dimensions={0} | all-to-all | bytes 2097152 | tf_op jit(solution)/shard_map/all_to_all | solution.py:125
  254.0 0.8 copy.69
  254.8 0.6 copy.80
  255.5 2.6 collective-permute-done.1
  258.1 1.0 copy.97
  (49 shorter events, 2.9 us)
Async XLA Ops:
  6.5 16.9 %copy-start.2 = (bf16[1,256,2048]{2,1,0:T(8,128)(2,1)S(1)}, bf16[1,256,2048]{2,1,0:T(8,128)(2,1)}, u32[]{:S(2)}) copy-start(bf16[1,256,2048]{2,1,0:T(8,128)(2,1)} %param.13) | copy-start | bytes 3145732
  6.5 73.5 %all-gather.7.cloned.1.call-start = ((), (), s32[]{:S(2)}) async-start(), calls=%async_computation.4 | async-start | bytes 5242880 | tf_op jit(solution)/shard_map/all_gather | solution.py:19
  8.1 13.3 %collective-permute-start = (bf16[3,3072]{1,0:T(4,128)(2,1)S(1)}, bf16[3,3072]{1,0:T(4,128)(2,1)S(1)}, u32[]{:S(2)}, u32[]{:S(2)}) collective-permute-start(bf16[3,3072]{1,0:T(4,128)(2,1)S(1)} %pad_maximum_fusion.3), channel_id=1, source_target_pairs={{0,4},{4,8},{8,12},{1,5},{5,9},{9,13},{2,6},{6,10},{10,14},{3,7},{... | collective-permute-start | bytes 55304 | tf_op jit(solution)/shard_map/ppermute | solution.py:13
  25.5 1.6 copy-start.7
  25.5 2.3 copy-start
  26.9 10.6 %copy-start.6 = (f32[1,4,512]{2,1,0:T(4,128)S(1)}, f32[1,4,512]{2,1,0:T(4,128)}, u32[]{:S(2)}) copy-start(f32[1,4,512]{2,1,0:T(4,128)} %param.20) | copy-start | bytes 24580
  26.9 10.6 %copy-start.3 = (bf16[1,256,512]{2,1,0:T(8,128)(2,1)S(1)}, bf16[1,256,512]{2,1,0:T(8,128)(2,1)}, u32[]{:S(2)}) copy-start(bf16[1,256,512]{2,1,0:T(8,128)(2,1)} %param.15) | copy-start | bytes 786436
  27.0 118.6 %all-gather.5.cloned.1.call-start = ((), (), s32[]{:S(2)}) async-start(), calls=%async_computation.2 | async-start | bytes 5242880 | tf_op jit(solution)/shard_map/all_gather | solution.py:118
  80.0 3.0 %copy-start.1 = (f32[1,256,2048]{1,2,0:T(8,128)S(1)}, f32[1,256,2048]{1,2,0:T(8,128)}, u32[]{:S(2)}) copy-start(f32[1,256,2048]{1,2,0:T(8,128)} %copy.67) | copy-start | bytes 6291460
  80.0 3.0 %copy-start.4 = (f32[256,2,16]{0,2,1:T(8,128)S(1)}, f32[256,2,16]{0,2,1:T(8,128)}, u32[]{:S(2)}) copy-start(f32[256,2,16]{0,2,1:T(8,128)} %get-tuple-element.7) | copy-start | bytes 98308
  90.2 0.9 copy-start.5
  92.9 143.5 %reduce-scatter.2.cloned.1.call-start = ((), (), s32[]{:S(2)}) async-start(), calls=%async_computation.3 | async-start | bytes 5242880 | tf_op jit(solution)/shard_map/reduce_scatter | solution.py:124
  255.4 2.7 %collective-permute-start.1 = (bf16[64,8192]{1,0:T(8,128)(2,1)S(1)}, bf16[64,8192]{1,0:T(8,128)(2,1)S(1)}, u32[]{:S(2)}, u32[]{:S(2)}) collective-permute-start(bf16[64,8192]{1,0:T(8,128)(2,1)S(1)} %bitcast.104), channel_id=1, source_target_pairs={{16,0},{0,16},{17,1},{1,17},{18,2},{2,18},{19,3},{3,19},{20,4},{4,... | collective-permute-start | bytes 3145736 | tf_op jit(solution)/shard_map/ppermute | solution.py:30
Sparse Core Ops, SparseCore 0:
  27.1 52.8 all-gather.6
  93.0 52.5 all-gather.4
  159.6 76.7 reduce-scatter.1
where the time goes:
time: 266 us
  waiting for transfers between devices  174 us (65%)
  blocking collectives  25.7 us (10%)
  matrix products  22.9 us (9%)
  local copies, waits for them, and re-layouts  13.5 us (5%)
  between operations  13.4 us (5%)
  other arithmetic  11 us (4%)
  starting transfers between devices  5.03 us (2%)
    reduce_scatter x1, waiting for transfers between devices, per_device(): summed = lax.psum_scatter(terms, 'head', scatter_dimension=1, tiled=True)  77 us
    all_gather x1, waiting for transfers between devices, per_device(): lax.all_gather(hidden, 'seq', axis=0, tiled=True)  52.7 us
    all_gather x1, waiting for transfers between devices, entering(): blocks = lax.all_gather(block.astype(jnp.bfloat16), axis)  41.8 us
    all_to_all x1, blocking collectives, per_device(): lax.all_to_all(summed, 'seq', split_axis=0, concat_axis=2, tiled=True)  17.6 us
    dot_general x1, matrix products, per_device(): jnp.dot(lax.all_gather(hidden, 'seq', axis=0, tiled=True), local_weight,...  13.8 us
    all_gather x1, blocking collectives, entering(): decays = lax.all_gather(decay, axis)  8.08 us
  transfers between devices with their start and end apart: 5, of which 4 were waited for; matrix products, arithmetic and copies ran while one was open for 4% of the time, Pallas kernels for 0%

commit v1 on v0

--- a/solution.py
+++ b/solution.py
@@ -53,6 +53,13 @@
     norm_gain,
     out_weight,
 ):
+
+    def outputs_list(base_x):
+        copies = []
+        for _ in range(lax.axis_size("seq")):
+            copies.append(base_x)
+        return jnp.concatenate(lax.all_to_all(jnp.stack(copies, 0), "seq", 0, 0), 0)
+
     x_local = x_in[0]
     b_local = b_in[0]
     c_local = c_in[0]
@@ -114,11 +121,7 @@
     inverse_rms = lax.rsqrt(jnp.mean(gated * gated, axis=2, keepdims=True) + epsilon)
     hidden = ((gated * inverse_rms).reshape(length, x_cols) * norm_gain[0]).astype(jnp.bfloat16)
     local_weight = out_weight[0]
-    terms = jnp.dot(
-        lax.all_gather(hidden, "seq", axis=0, tiled=True),
-        local_weight,
-        preferred_element_type=jnp.float32,
-    )
+    terms = jnp.dot(outputs_list(hidden), local_weight, preferred_element_type=jnp.float32)
     shards = lax.axis_size("seq")
     terms = terms.astype(jnp.bfloat16).reshape(shards, length, local_weight.shape[1])
     summed = lax.psum_scatter(terms, "head", scatter_dimension=1, tiled=True)

time: 266 us -> 268 us (level)
  waiting for transfers between devices: 174 us -> 120 us
  blocking collectives: 25.7 us -> 76.3 us
  local copies, waits for them, and re-layouts: 13.5 us -> 19.8 us
    all_gather x1 -> x0, waiting for transfers between devices: 52.7 us -> none  [per_device(): lax.all_gather(hidden, 'seq', axis=0, tiled=True)]
    all_to_all x0 -> x1, blocking collectives: none -> 50.7 us  [outputs_list(): return jnp.concatenate(lax.all_to_all(jnp.stack(copies, 0), 'seq', 0, 0), 0)]
    mul x1 -> x2, local copies, waits for them, and re-layouts: 0.61 us -> 5.99 us  [per_device(): gated * inverse_rms]
    dot_general x1, matrix products: 13.8 us -> 10.4 us  [per_device(): jnp.dot(outputs_list(hidden), local_weight, preferred_element_type=jnp.fl...]
  transfers between devices with their start and end apart: 5 -> 4, of which waited for: 4 -> 3; matrix products, arithmetic and copies ran while one was open for 4% -> 4% of each run, Pallas kernels for 0% -> 0%
where the time goes in v1:
time: 268 us; the launch traced here: 267 us
  waiting for transfers between devices  120 us (45%)
  blocking collectives  76.3 us (28%)
  matrix products  20.6 us (8%)
  local copies, waits for them, and re-layouts  19.8 us (7%)
  between operations  13.7 us (5%)
  other arithmetic  11.7 us (4%)
  starting transfers between devices  4.99 us (2%)
    reduce_scatter x1, waiting for transfers between devices, per_device(): summed = lax.psum_scatter(terms, 'head', scatter_dimension=1, tiled=True)  76.4 us
    all_to_all x1, blocking collectives, outputs_list(): return jnp.concatenate(lax.all_to_all(jnp.stack(copies, 0), 'seq', 0, 0), 0)  50.7 us
    all_gather x1, waiting for transfers between devices, entering(): blocks = lax.all_gather(block.astype(jnp.bfloat16), axis)  41.2 us
    all_to_all x1, blocking collectives, per_device(): lax.all_to_all(summed, 'seq', split_axis=0, concat_axis=2, tiled=True)  17.6 us
    dot_general x1, matrix products, per_device(): jnp.dot(outputs_list(hidden), local_weight, preferred_element_type=jnp.fl...  10.4 us
    all_gather x1, blocking collectives, entering(): decays = lax.all_gather(decay, axis)  8.09 us
    mul x2, local copies, waits for them, and re-layouts, per_device(): gated * inverse_rms  5.99 us
  transfers between devices with their start and end apart: 4, of which 3 were waited for; matrix products, arithmetic and copies ran while one was open for 4% of the time, Pallas kernels for 0%

profile of v1, /device:TPU:0, one launch (start us, length us, event | category | flops | bytes accessed | tf_op | source)
XLA Modules:
  0.0 267.4 jit_solution(13109016504884996876)
XLA Ops:
  6.5 0.9 slice_bitcast_fusion
  7.4 0.7 slice_bitcast_fusion.1
  8.1 4.9 %collective-permute-start = (bf16[3,3072]{1,0:T(4,128)(2,1)S(1)}, bf16[3,3072]{1,0:T(4,128)(2,1)S(1)}, u32[]{:S(2)}, u32[]{:S(2)}) collective-permute-start(bf16[3,3072]{1,0:T(4,128)(2,1)S(1)} %pad_maximum_fusion.3), channel_id=1, source_target_pairs={{0,4},{4,8},{8,12},{1,5},{5,9},{9,13},{2,6},{6,10},{10,14},{3,7},{... | collective-permute-start | bytes 55304 | tf_op jit(solution)/shard_map/ppermute | solution.py:13
  13.0 0.7 negate_bitcast_fusion
  14.2 1.3 reduce.9
  15.6 0.8 squeeze.26
  16.4 0.7 fusion.41
  18.2 0.9 fusion.44
  19.2 1.4 multiply_bitcast_fusion
  20.6 0.9 fusion.47
  21.5 1.9 multiply_convert_fusion.6
  23.4 0.8 reshape.186
  24.2 1.5 multiply_convert_fusion.3
  26.2 2.5 convolution_convert_fusion
  28.8 0.6 reduce.10
  30.0 1.6 copy.67
  31.6 8.1 %all-gather = f32[8,16,1]{1,2,0:T(1,128)S(1)} all-gather(f32[2,16,1]{1,2,0:T(1,128)S(1)} %bitcast.106), channel_id=2, replica_groups=mesh['section'=2,'seq'=4,'head'=4] {'seq'}, dimensions={0}, use_global_device_ids=true | all-gather | bytes 640 | tf_op jit(solution)/shard_map/all_gather | solution.py:18
  40.5 41.2 %all-gather.4.cloned.1.call-done = bf16[8,16,64,256]{3,2,1,0:T(8,128)(2,1)} async-done(((bf16[2,16,64,256]{3,2,1,0:T(8,128)(2,1)}), bf16[8,16,64,256]{3,2,1,0:T(8,128)(2,1)}) %all-gather.4.cloned.1.call-update) | async-done | bytes 4194320 | tf_op jit(solution)/shard_map/all_gather | solution.py:19
  81.7 3.0 %fusion.24 = f32[2,16,64,256]{3,2,1,0:T(8,128)S(1)} fusion(bf16[8,16,64,256]{3,2,1,0:T(8,128)(2,1)} %all-gather.4.cloned.1.call-done, f32[2,16]{1,0:T(2,128)S(1)} %bitcast.109, f32[2,16]{1,0:T(2,128)S(1)} %bitcast.108, f32[2,16]{1,0:T(2,128)S(1)} %bitcast.107, pred[]{:T(512)S(6)} %gt.11, pred[]{:T(512)S(6)} %gt.10, pred[]{:T(512)S(6)} %gt.9, ...), kind=kOutput, calls=%fused_computation.35 | convolution fusion | flops 274726912 | bytes 5505411 | tf_op jit(solution)/shard_map/tgn,gjpn->tgjp/dot_general | solution.py:113
  84.7 4.5 %multiply_reduce_fusion = (f32[256,2]{0,1:T(2,128)S(1)}, f32[256,2,16,64]{0,3,2,1:T(8,128)}) fusion(f32[256,2,16,64]{0,3,2,1:T(8,128)S(1)} %bitcast.80, bf16[256,2,16,64]{0,3,2,1:T(8,128)(2,1)S(1)} %bitcast.84, f32[2,16]{1,0:T(2,128)S(1)} %copy-done.8, f32[256,2,16]{0,2,1:T(8,128)S(1)} %copy-done.4, f32[2,16,64,256]{3,2,1,0:T(8,128)S(1)} %fusion.24, ...), kind=kOutput, calls=%fused_computation.26 | convolution fusion | flops 287309312 | bytes 8030336 | tf_op jit(solution)/shard_map/gjtu,ugjp->tgjp/dot_general | solution.py:102
  89.2 1.9 copy.66
  91.3 2.0 mul.328
  93.3 4.0 %mul.329 = f32[1,256,2048]{2,1,0:T(8,128)} reshape(f32[256,2,1024]{2,1,0:T(2,128)} %mul.328) | data formatting | bytes 4194304 | tf_op jit(solution)/shard_map/mul | solution.py:122
  97.3 2.5 fusion.29
  100.3 50.7 %all_to_all.20 = bf16[4,256,2048]{2,1,0:T(8,128)(2,1)S(1)} all-to-all(bf16[4,256,2048]{2,1,0:T(8,128)(2,1)S(1)} %stack.10), channel_id=1, replica_groups=mesh['section'=2,'seq'=4,'head'=4] {'seq'}, dimensions={0} | all-to-all | bytes 8388608 | tf_op jit(solution)/shard_map/all_to_all | solution.py:61
  151.0 10.4 %fusion.9 = bf16[1024,2048]{1,0:T(8,128)(2,1)} fusion(bf16[1024,2048]{1,0:T(8,128)(2,1)S(1)} %bitcast.75, bf16[1,2048,2048]{2,1,0:T(8,128)(2,1)S(1)} %bitcast.112), kind=kOutput, calls=%fused_computation.10 | convolution fusion | flops 8592031744 | bytes 16777216 | tf_op jit(solution)/shard_map/dot_general | solution.py:124
  161.4 76.4 %reduce-scatter.2.cloned.1.call-done = bf16[4,64,2048]{2,1,0:T(8,128)(2,1)} async-done(((bf16[4,256,2048]{2,1,0:T(8,128)(2,1)}), bf16[4,64,2048]{2,1,0:T(8,128)(2,1)}) %reduce-scatter.2.cloned.1.call-update) | async-done | bytes 1048592 | tf_op jit(solution)/shard_map/reduce_scatter | solution.py:127
  237.8 17.6 %all_to_all.21 = bf16[4,64,2048]{2,1,0:T(8,128)(2,1)S(1)} all-to-all(bf16[4,64,2048]{2,1,0:T(8,128)(2,1)} %reduce-scatter.2.cloned.1.call-done), channel_id=1, replica_groups=mesh['section'=2,'seq'=4,'head'=4] {'seq'}, dimensions={0} | all-to-all | bytes 2097152 | tf_op jit(solution)/shard_map/all_to_all | solution.py:128
  255.4 0.8 copy.69
  256.2 0.6 copy.79
  256.9 2.6 collective-permute-done.1
  259.6 1.0 copy.96
  (55 shorter events, 4.4 us)
Async XLA Ops:
  6.5 17.6 %copy-start.2 = (bf16[1,256,2048]{2,1,0:T(8,128)(2,1)S(1)}, bf16[1,256,2048]{2,1,0:T(8,128)(2,1)}, u32[]{:S(2)}) copy-start(bf16[1,256,2048]{2,1,0:T(8,128)(2,1)} %param.13) | copy-start | bytes 3145732
  6.5 75.2 %all-gather.4.cloned.1.call-start = ((), (), s32[]{:S(2)}) async-start(), calls=%async_computation.4 | async-start | bytes 5242880 | tf_op jit(solution)/shard_map/all_gather | solution.py:19
  8.1 13.3 %collective-permute-start = (bf16[3,3072]{1,0:T(4,128)(2,1)S(1)}, bf16[3,3072]{1,0:T(4,128)(2,1)S(1)}, u32[]{:S(2)}, u32[]{:S(2)}) collective-permute-start(bf16[3,3072]{1,0:T(4,128)(2,1)S(1)} %pad_maximum_fusion.3), channel_id=1, source_target_pairs={{0,4},{4,8},{8,12},{1,5},{5,9},{9,13},{2,6},{6,10},{10,14},{3,7},{... | collective-permute-start | bytes 55304 | tf_op jit(solution)/shard_map/ppermute | solution.py:13
  26.2 2.6 copy-start.7
  26.2 3.8 %copy-start = (bf16[1,256,2048]{2,1,0:T(8,128)(2,1)S(1)}, bf16[1,256,2048]{2,1,0:T(8,128)(2,1)}, u32[]{:S(2)}) copy-start(bf16[1,256,2048]{2,1,0:T(8,128)(2,1)} %param.16) | copy-start | bytes 3145732
  28.7 11.1 %copy-start.6 = (f32[1,4,512]{2,1,0:T(4,128)S(1)}, f32[1,4,512]{2,1,0:T(4,128)}, u32[]{:S(2)}) copy-start(f32[1,4,512]{2,1,0:T(4,128)} %param.20) | copy-start | bytes 24580
  28.7 11.1 %copy-start.3 = (bf16[1,256,512]{2,1,0:T(8,128)(2,1)S(1)}, bf16[1,256,512]{2,1,0:T(8,128)(2,1)}, u32[]{:S(2)}) copy-start(bf16[1,256,512]{2,1,0:T(8,128)(2,1)} %param.15) | copy-start | bytes 786436
  28.7 209.1 %reduce-scatter.2.cloned.1.call-start = ((), (), s32[]{:S(2)}) async-start(), calls=%async_computation.3 | async-start | bytes 5242880 | tf_op jit(solution)/shard_map/reduce_scatter | solution.py:127
  81.7 3.0 %copy-start.1 = (f32[1,256,2048]{1,2,0:T(8,128)S(1)}, f32[1,256,2048]{1,2,0:T(8,128)}, u32[]{:S(2)}) copy-start(f32[1,256,2048]{1,2,0:T(8,128)} %copy.67) | copy-start | bytes 6291460
  81.7 3.0 %copy-start.4 = (f32[256,2,16]{0,2,1:T(8,128)S(1)}, f32[256,2,16]{0,2,1:T(8,128)}, u32[]{:S(2)}) copy-start(f32[256,2,16]{0,2,1:T(8,128)} %get-tuple-element.7) | copy-start | bytes 98308
  81.7 3.0 %copy-start.8 = (f32[2,16]{1,0:T(2,128)S(1)}, f32[2,16]{1,0:T(2,128)}, u32[]{:S(2)}) copy-start(f32[2,16]{1,0:T(2,128)} %mul.320) | copy-start | bytes 388
  93.3 4.0 %copy-start.5 = (f32[1,2048]{1,0:T(1,128)S(1)}, f32[1,2048]{1,0:T(1,128)}, u32[]{:S(2)}) copy-start(f32[1,2048]{1,0:T(1,128)} %param.24) | copy-start | bytes 24580
  97.3 53.7 %slice-start = ((s8[8388608]{0:T(1024)(128)(4,1)}), s8[4194304]{0:T(1024)(128)(4,1)S(1)}, s32[]{:S(2)}) async-start(s8[8388608]{0:T(1024)(128)(4,1)} %bitcast.111), calls=%async_computation.5 | async-start | bytes 8388608
  99.8 51.2 %slice-start.1 = ((s8[8388608]{0:T(1024)(128)(4,1)}), s8[4194304]{0:T(1024)(128)(4,1)S(1)}, s32[]{:S(2)}) async-start(s8[8388608]{0:T(1024)(128)(4,1)} %bitcast.111), calls=%async_computation.6 | async-start | bytes 8388608
  256.9 2.7 %collective-permute-start.1 = (bf16[64,8192]{1,0:T(8,128)(2,1)S(1)}, bf16[64,8192]{1,0:T(8,128)(2,1)S(1)}, u32[]{:S(2)}, u32[]{:S(2)}) collective-permute-start(bf16[64,8192]{1,0:T(8,128)(2,1)S(1)} %bitcast.85), channel_id=1, source_target_pairs={{16,0},{0,16},{17,1},{1,17},{18,2},{2,18},{19,3},{3,19},{20,4},{4,... | collective-permute-start | bytes 3145736 | tf_op jit(solution)/shard_map/ppermute | solution.py:30
Sparse Core Ops, SparseCore 0:
  28.8 52.8 all-gather.3
  161.6 76.2 reduce-scatter.1
